TPU v7x, 32 devices: a whole 2x2x4 slice. The times are simulated.
32 devices in a mesh: groups: 2 (over x), row: 16 (over z, y, core).
Axes of the slice: x: 2, y: 2, z: 4, core: 2. Of those that a mesh axis runs over, the one named last changes fastest.
Arguments:
- elevation: float32 [512, 8192], P(('groups', 'row')), parts along dimension 0, may hold values from -2048 to 4096
- bin_index: int32 [512, 8192], P(('groups', 'row')), parts along dimension 0, may hold values from 0 to 1023, as said below
- ranks: int32 [4], P('groups'), parts along dimension 0, may hold values from 20971 to 2076128, as said below
Outputs:
- shaded: float32 [512, 8192], P(('groups', 'row')), parts along dimension 0
There are 2 independent parts, one for each index of `groups`. A program takes and returns all parts, laid end to end along the dimension named above; each array names one. Nothing has to cross between parts.
Inputs may be any that keep to these rules, and one draw needn't show every extreme that they name: The bins have fixed edges: a cell with 0 < bin_index < 1023 has an elevation at or above 2 bin_index and below 2 bin_index + 2; bin 0 holds every elevation below 2 and bin 1024 - 1 every elevation at or above 2046. `ranks`: the first entry lies below 104857 and the second at or above 1992245.
All inputs are finite; a program needn't handle non-finite values.
Results may differ from a plain program's by a relative error of at most 0.0049.
Values sent between devices are 32-bit elements; how exact they have to be, the bound alone decides.
A program may use at most 64 MiB of HBM per device.

v0:
```python
import jax
import jax.numpy as jnp
from jax import lax
from jax.sharding import PartitionSpec as P

BINS = 1024


binomial = (1.0 / 64, 6.0 / 64, 15.0 / 64, 20.0 / 64, 15.0 / 64, 6.0 / 64, 1.0 / 64)
zfactor = 200.0
cos_zenith = 0.70710678
sin_zenith = 0.70710678
light_x = -0.70710678
light_y = 0.70710678
low_bins = 32


def padded_2(cells, sides, width):
    for axis, dim in sides:
        count = lax.axis_size(axis)
        ends = count - 1
        head = lax.slice_in_dim(cells, 0, width, axis=dim)
        tail = lax.slice_in_dim(cells, cells.shape[dim] - width, cells.shape[dim], axis=dim)
        cells = jnp.concatenate(
            [
                lax.ppermute(tail, axis, [(i, (i + 1) % count) for i in range(ends)]),
                cells,
                lax.ppermute(head, axis, [((i + 1) % count, i) for i in range(ends)]),
            ],
            axis=dim,
        )
    return cells


def filter_cols(padded):
    width = padded.shape[1] - 6
    total = binomial[0] * padded[:, 0:width]
    for offset in range(1, 7):
        total = total + binomial[offset] * padded[:, offset : offset + width]
    return total


def filter_rows(padded):
    height = padded.shape[0] - 6
    total = binomial[0] * padded[0:height, :]
    for offset in range(1, 7):
        total = total + binomial[offset] * padded[offset : offset + height, :]
    return total


def shade(smooth, span):
    height = smooth.shape[0] - 2
    width = smooth.shape[1] - 2

    def window(drow, dcol):
        return smooth[drow : drow + height, dcol : dcol + width]

    east = window(0, 2) + 2.0 * window(1, 2) + window(2, 2)
    west = window(0, 0) + 2.0 * window(1, 0) + window(2, 0)
    south = window(2, 0) + 2.0 * window(2, 1) + window(2, 2)
    north = window(0, 0) + 2.0 * window(0, 1) + window(0, 2)
    scale = zfactor / (8.0 * span)
    grad_x = (east - west) * scale
    grad_y = (south - north) * scale
    light = (cos_zenith - sin_zenith * (light_x * grad_x + light_y * grad_y)) * lax.rsqrt(
        1.0 + grad_x * grad_x + grad_y * grad_y
    )
    return jnp.maximum(light, 0.0)


def one_hots(block, upper_count):
    upper_idx = block // low_bins
    lower_idx = block % low_bins
    upper_hot = (upper_idx[None, :] == lax.broadcasted_iota(jnp.int32, (upper_count, 1), 0)).astype(
        jnp.bfloat16
    )
    lower_hot = (lower_idx[None, :] == lax.broadcasted_iota(jnp.int32, (low_bins, 1), 0)).astype(
        jnp.bfloat16
    )
    return (upper_hot, lower_hot)


def body(elevation, bin_index, ranks):
    height = elevation.shape[0]
    width = elevation.shape[1]
    upper_count = BINS // low_bins
    blocked = bin_index.reshape(height // 4, 4 * width)

    def count_block(carry, block):
        upper_hot, lower_hot = one_hots(block, upper_count)
        part_counts = lax.dot_general(
            upper_hot, lower_hot, (((1,), (1,)), ((), ())), preferred_element_type=jnp.float32
        )
        return (carry + part_counts, None)

    local_counts, unused = lax.scan(
        count_block, jnp.zeros((upper_count, low_bins), jnp.float32), blocked
    )
    local_counts = local_counts.reshape(BINS)
    local_max = jnp.max(elevation)
    local_min = jnp.min(elevation)
    counts = lax.psum(local_counts, "row")
    highest, neg_lowest = lax.pmax((local_max, -local_min), "row")
    lowest = -neg_lowest
    span = highest - lowest
    cumulative = jnp.cumsum(counts.astype(jnp.int32), dtype=jnp.int32)
    table = jnp.clip(
        (cumulative - ranks[0]).astype(jnp.float32) / (ranks[1] - ranks[0]).astype(jnp.float32),
        0.0,
        1.0,
    ).astype(jnp.bfloat16)
    stretch = jnp.take(table.astype(jnp.float32), bin_index, axis=0)
    extended = padded_2(elevation, (("row", 0),), 4)
    smooth = filter_rows(filter_cols(jnp.pad(extended, ((0, 0), (4, 4)))))
    light = shade(smooth, span)
    return stretch * (0.5 + light)


def solution(mesh):
    in_specs = (P(("groups", "row"), None), P(("groups", "row"), None), P("groups"))
    out_specs = P(("groups", "row"), None)
    return jax.shard_map(body, mesh=mesh, in_specs=in_specs, out_specs=out_specs, check_vma=False)
```

profile of v0, /device:TPU:0, one launch (start us, length us, event | category | flops | bytes accessed | tf_op | source)
XLA Modules:
  0.0 617.2 jit_solution(2597587852757013401)
XLA Ops:
  0.0 0.0 copy-start
  0.0 1.8 fusion.31
  1.8 3.1 collective-permute-start
  4.9 1.3 collective-permute-start.1
  6.2 1.8 fusion.30
  8.0 0.0 copy-done
  8.0 0.0 copy-start.3
  8.0 0.3 reshape.30
  8.3 0.1 fusion.29
  8.4 0.2 copy-done.3
  8.6 0.6 fusion.32
  11.2 36.3 %all-reduce.1 = (f32[]{:T(128)}, f32[]{:T(128)}) all-reduce(f32[]{:T(128)} %get-tuple-element.63, f32[]{:T(128)S(6)} %neg.6), channel_id=1, replica_groups=mesh['groups'=2,'row'=16] {'row'}, use_global_device_ids=true, to_apply=%region_6.7 | all-reduce | flops 2 | bytes 16 | tf_op jit(solution)/shard_map/pmax | solution.py:103
  48.2 10.7 %while.13 = (s32[]{:T(128)}, f32[32,32]{1,0:T(8,128)S(1)}, s32[4,32768]{1,0:T(4,128)S(1)}, s32[]{:T(128)}, s32[]{:T(128)}) while((s32[]{:T(128)}, f32[32,32]{1,0:T(8,128)S(1)}, s32[4,32768]{1,0:T(4,128)S(1)}, s32[]{:T(128)}, s32[]{:T(128)}) %tuple.36), condition=%wide.region_1.2_spmd.clone, body=%wide.region_0.1_spmd.clone.sunk | while | flops 69863424 | bytes 3022931 | solution.py:96
  48.2 0.6 and_select_fusion.4
  48.9 0.2 and_select_fusion.5
  49.1 0.5 iota_compare_fusion.20
  49.6 1.3 fusion.37
  50.9 0.6 and_select_fusion.4
  51.6 0.2 and_select_fusion.5
  51.7 0.5 iota_compare_fusion.20
  52.3 1.3 fusion.37
  53.6 0.6 and_select_fusion.4
  54.2 0.2 and_select_fusion.5
  54.4 0.5 iota_compare_fusion.20
  55.0 1.3 fusion.37
  56.3 0.6 and_select_fusion.4
  56.9 0.2 and_select_fusion.5
  57.1 0.5 iota_compare_fusion.20
  57.7 1.3 fusion.37
  58.9 0.1 reshape.31
  59.0 29.5 %psum.7 = f32[1024]{0:T(1024)S(1)} all-reduce(f32[1024]{0:T(1024)S(1)} %reshape.31), channel_id=1, replica_groups=mesh['groups'=2,'row'=16] {'row'}, use_global_device_ids=true, to_apply=%region_2.3 | all-reduce | flops 1024 | bytes 8192 | tf_op jit(solution)/shard_map/psum | solution.py:102
  88.5 0.3 reduce-window.9
  88.8 0.1 slice.90
  88.9 0.1 slice_reduce_fusion
  89.0 0.1 copy.4
  89.1 0.1 broadcast_clamp_fusion
  89.2 0.7 bitcast_convert_fusion
  89.9 520.8 %gather_fusion = f32[131072]{0:T(1024)S(1)} fusion(f32[1024]{0:T(1024)S(1)} %bitcast_convert_fusion, s32[131072]{0:T(1024)S(1)} %broadcast_clamp_fusion), kind=kCustom, calls=%fused_computation | custom fusion | bytes 1572864 | tf_op jit(solution)/shard_map/jit(_take)/gather | solution.py:112
  610.7 0.0 copy-start.2
  610.7 0.1 reshape.40
  611.5 0.0 collective-permute-done
  611.6 0.0 collective-permute-done.1
  611.6 0.2 copy-done.2
  611.8 1.4 select_maximum_fusion
  613.1 1.3 fusion.10
  614.4 0.0 copy-start.1
  614.5 0.6 fusion.4
  615.1 0.4 copy-done.1
  615.5 1.7 add_multiply_fusion
  (3 shorter events, 0.0 us)
Async XLA Ops:
  0.0 8.0 %copy-start = (s32[16,8192]{1,0:T(8,128)S(1)}, s32[16,8192]{1,0:T(8,128)}, u32[]{:S(2)}) copy-start(s32[16,8192]{1,0:T(8,128)} %param.6) | copy-start | bytes 1572868
  1.8 609.7 %collective-permute-start = (f32[4,8192]{1,0:T(4,128)}, f32[4,8192]{1,0:T(4,128)}, u32[]{:S(2)}, u32[]{:S(2)}) collective-permute-start(f32[4,8192]{1,0:T(4,128)} %get-tuple-element.74), channel_id=1, source_target_pairs={{0,1},{1,2},{2,3},{3,4},{4,5},{5,6},{6,7},{7,8},{8,9},{9,10},{10,1... | collective-permute-start | bytes 393224 | tf_op jit(solution)/shard_map/ppermute | solution.py:26
  4.9 606.7 %collective-permute-start.1 = (f32[4,8192]{1,0:T(4,128)}, f32[4,8192]{1,0:T(4,128)}, u32[]{:S(2)}, u32[]{:S(2)}) collective-permute-start(f32[4,8192]{1,0:T(4,128)} %get-tuple-element.75), channel_id=1, source_target_pairs={{1,0},{2,1},{3,2},{4,3},{5,4},{6,5},{7,6},{8,7},{9,8},{10,9},{11,1... | collective-permute-start | bytes 393224 | tf_op jit(solution)/shard_map/ppermute | solution.py:28
  8.0 0.7 copy-start.3
  610.7 1.0 copy-start.2
  614.4 1.0 copy-start.1
where the time goes:
time: 618 us; the launch traced here: 617 us
  local copies, waits for them, and re-layouts  525 us (85%)
  blocking collectives  65.8 us (11%)
  other arithmetic  13.4 us (2%)
    gather x2, local copies, waits for them, and re-layouts, body(): stretch = jnp.take(table.astype(jnp.float32), bin_index, axis=0)  521 us
    pmax x1, blocking collectives, body(): highest, neg_lowest = lax.pmax((local_max, -local_min), 'row')  36.3 us
    psum x1, blocking collectives, body(): counts = lax.psum(local_counts, 'row')  29.5 us
  transfers between devices with their start and end apart: 2, of which 0 were waited for; matrix products, arithmetic and copies ran while one was open for 87% of the time, Pallas kernels for 0%

commit v1 on v0

v1 whole, which is shorter than its diff:
```python
import functools

import jax
import jax.numpy as jnp
from jax import lax
from jax.experimental import pallas as pl
from jax.experimental.pallas import tpu as pltpu
from jax.sharding import PartitionSpec as P

BINS = 1024
zfactor = 200.0
cos_zenith = 0.70710678
sin_zenith = 0.70710678
light_x = -0.70710678
light_y = 0.70710678
LANES = 128
HALO = 4
PAD = 128
SMOOTH = (1.0, 8.0, 28.0, 56.0, 70.0, 56.0, 28.0, 8.0, 1.0)
SLOPE = (-1.0, -6.0, -14.0, -14.0, 0.0, 14.0, 14.0, 6.0, 1.0)
UPPER = 16
LOWER = BINS // UPPER


def bins_of(cells):
    return jnp.floor(jnp.clip(cells * 0.5, 0.0, float(BINS - 1)))


def row_weights(weights, height):
    depth = 3 * (height + 8) + 8
    row = lax.broadcasted_iota(jnp.int32, (height, depth), 0)
    col = lax.broadcasted_iota(jnp.int32, (height, depth), 1)
    own = lax.rem(col, height)
    edge = lax.rem(jnp.maximum(col - 3 * height, 0), 8)
    edge = jnp.where(edge < HALO, height + edge, edge - 8)
    source = jnp.where(col < 3 * height, own, edge)
    source = jnp.where(col < 3 * (height + 8), source, 4 * height)
    delta = source - row
    out = jnp.zeros((height, depth), jnp.float32)
    for k, weight in enumerate(weights):
        out = jnp.where(delta == k - HALO, weight, out)
    return out.astype(jnp.bfloat16)


def split3(cells):
    first = cells.astype(jnp.bfloat16).astype(jnp.float32)
    rest = cells - first
    second = rest.astype(jnp.bfloat16).astype(jnp.float32)
    return first, second, rest - second


def stacked(cells):
    halo = split3(cells[0:8])
    own = split3(cells[8:])
    return jnp.concatenate([*own, *halo, jnp.zeros_like(halo[0])], axis=0).astype(jnp.bfloat16)


def kernel(n, chunk, ranks_ref, elev_ref, out_ref, cells, upper, lower, send, recv, slope_x, slope_y,
           result, in_sem, halo_send, halo_recv, send_sem, recv_sem, out_sem):
    me = lax.axis_index("row")
    height, width = elev_ref.shape
    chunks = width // chunk
    inner = pl.ds(PAD, width)

    load = pltpu.make_async_copy(elev_ref, cells.at[pl.ds(8, height), inner], in_sem)
    load.start()

    barrier = pltpu.get_barrier_semaphore()

    def greet(k, carry):
        pl.semaphore_signal(barrier, inc=1, device_id={"row": lax.rem(me + k, n)},
                            device_id_type=pl.DeviceIdType.MESH)
        return carry

    lax.fori_loop(1, n, greet, 0)

    zeros = jnp.zeros((height + 8, PAD), jnp.float32)
    cells[:, pl.ds(0, PAD)] = zeros
    cells[:, pl.ds(PAD + width, PAD)] = zeros

    @pl.when(me == 0)
    def _():
        cells[4:8, inner] = jnp.zeros((4, width), jnp.float32)

    @pl.when(me == n - 1)
    def _():
        cells[0:4, inner] = jnp.zeros((4, width), jnp.float32)

    load.wait()
    pl.semaphore_wait(barrier, n - 1)

    down = pltpu.make_async_remote_copy(
        src_ref=cells.at[pl.ds(8 + height - HALO, HALO), inner], dst_ref=cells.at[pl.ds(4, HALO), inner],
        send_sem=halo_send.at[0], recv_sem=halo_recv.at[0],
        device_id={"row": lax.rem(me + 1, n)}, device_id_type=pl.DeviceIdType.MESH)
    up = pltpu.make_async_remote_copy(
        src_ref=cells.at[pl.ds(8, HALO), inner], dst_ref=cells.at[pl.ds(0, HALO), inner],
        send_sem=halo_send.at[1], recv_sem=halo_recv.at[1],
        device_id={"row": lax.rem(me + n - 1, n)}, device_id_type=pl.DeviceIdType.MESH)

    @pl.when(me < n - 1)
    def _():
        down.start()

    @pl.when(me > 0)
    def _():
        up.start()

    def prepare(i, carry):
        top, bottom = carry
        at = pl.multiple_of(i * chunk, chunk)
        block = cells[pl.ds(8, height), pl.ds(at + PAD, chunk)]
        bins = bins_of(block)
        high = jnp.floor(bins * (1.0 / LOWER))
        upper[:, pl.ds(at, chunk)] = high
        lower[:, pl.ds(at, chunk)] = bins - high * LOWER
        for r in range(height // 8):
            for c in range(chunk // LANES):
                piece = block[8 * r : 8 * r + 8, c * LANES : (c + 1) * LANES]
                top, bottom = jnp.maximum(top, piece), jnp.minimum(bottom, piece)
        return top, bottom

    start = cells[8:16, PAD : PAD + LANES]
    top, bottom = lax.fori_loop(0, chunks, prepare, (start, start))

    urow = lax.broadcasted_iota(jnp.int32, (UPPER, chunk), 0)
    upper_iota = (2 * lax.rem(urow, 8) + urow // 8).astype(jnp.float32).astype(jnp.bfloat16)
    lower_iota = lax.broadcasted_iota(jnp.int32, (LOWER, chunk), 0).astype(jnp.float32).astype(jnp.bfloat16)

    def count(i, total):
        at = pl.multiple_of(i * chunk, chunk)
        for r in range(height):
            high = jnp.broadcast_to(upper[r : r + 1, pl.ds(at, chunk)], (UPPER, chunk)).astype(jnp.bfloat16)
            low = jnp.broadcast_to(lower[r : r + 1, pl.ds(at, chunk)], (LOWER, chunk)).astype(jnp.bfloat16)
            one, zero = jnp.ones((), jnp.bfloat16), jnp.zeros((), jnp.bfloat16)
            hot_u = jnp.where(high == upper_iota, one, zero)
            hot_l = jnp.where(low == lower_iota, one, zero)
            total = total + lax.dot_general(hot_u, hot_l, (((1,), (1,)), ((), ())),
                                            preferred_element_type=jnp.float32)
        return total

    total = lax.fori_loop(0, chunks, count, jnp.zeros((UPPER, LOWER), jnp.float32))
    counts = jnp.concatenate([total[0:8], total[8:16]], axis=1)
    send[0:8, :] = counts
    send[8:9, :] = jnp.max(top, axis=0, keepdims=True)
    send[9:10, :] = jnp.max(-bottom, axis=0, keepdims=True)

    def copy_to(k):
        return pltpu.make_async_remote_copy(
            src_ref=send, dst_ref=recv.at[k], send_sem=send_sem.at[k], recv_sem=recv_sem.at[k],
            device_id={"row": lax.rem(me + k, n)}, device_id_type=pl.DeviceIdType.MESH)

    def post(k, carry):
        copy_to(k).start()
        return carry

    lax.fori_loop(1, n, post, 0)

    @pl.when(me > 0)
    def _():
        down.wait_recv()

    @pl.when(me < n - 1)
    def _():
        up.wait_recv()

    smooth_w = row_weights(SMOOTH, height)
    slope_w = row_weights(SLOPE, height)
    span_w = chunk + 2 * PAD

    def stencil(i, carry):
        at = pl.multiple_of(i * chunk, chunk)
        x = cells[:, pl.ds(at, span_w)]
        for k in range(7):
            x = x + pltpu.roll(x, 1 if k % 2 else span_w - 1, 1)
        moved = pltpu.roll(x, 1, 1)
        rise = (x - moved)[:, PAD : PAD + chunk]
        level = (x + moved)[:, PAD : PAD + chunk]
        slope_x[:, pl.ds(at, chunk)] = jnp.dot(smooth_w, stacked(rise), preferred_element_type=jnp.float32)
        slope_y[:, pl.ds(at, chunk)] = jnp.dot(slope_w, stacked(level), preferred_element_type=jnp.float32)
        return carry

    lax.fori_loop(0, chunks, stencil, 0)

    def take(k, carry):
        copy_to(k).wait_recv()
        got = recv[k]
        return carry[0] + got[0:8], jnp.maximum(carry[1], got[8:10])

    counts, ends = lax.fori_loop(1, n, take, (send[0:8, :], send[8:10, :]))
    ends = jnp.max(ends, axis=1, keepdims=True)
    span = ends[0:1] + ends[1:2]
    scale = jnp.broadcast_to(zfactor / (8.0 * span) * (1.0 / 4096.0), (8, LANES))

    whole = counts.astype(jnp.int32)
    lane_in = lax.broadcasted_iota(jnp.int32, (LANES, LANES), 0)
    lane_out = lax.broadcasted_iota(jnp.int32, (LANES, LANES), 1)
    triangle = jnp.where(lane_in <= lane_out, 1.0, 0.0).astype(jnp.bfloat16)
    digits = jnp.concatenate([(whole & 255), ((whole >> 8) & 255), (whole >> 16), jnp.zeros_like(whole)],
                             axis=0).astype(jnp.float32).astype(jnp.bfloat16)
    sums = jnp.dot(digits, triangle, preferred_element_type=jnp.float32)
    within = sums[0:8] + 256.0 * sums[8:16] + 65536.0 * sums[16:24]
    before = jnp.zeros((1, 1), jnp.float32)
    rows = []
    first, second = ranks_ref[0], ranks_ref[1]
    for b in range(8):
        rows.append(before)
        before = before + within[b : b + 1, LANES - 1 : LANES]
    offsets = jnp.concatenate(rows, axis=0)
    cumulative = (within + offsets).astype(jnp.int32)
    divisor = jnp.full((8, LANES), second - first, jnp.int32).astype(jnp.float32)
    table = jnp.clip((cumulative - first).astype(jnp.float32) / divisor, 0.0, 1.0)
    table = table.astype(jnp.bfloat16).astype(jnp.float32)
    tables = [jnp.broadcast_to(table[b : b + 1], (8, LANES)) for b in range(8)]

    def out_copy(i):
        at = pl.multiple_of(i * chunk, chunk)
        where = (slice(None), pl.ds(at, chunk))
        return pltpu.make_async_copy(result.at[where], out_ref.at[where], out_sem.at[i])

    def finish(i, carry):
        at = pl.multiple_of(i * chunk, chunk)
        for r in range(height // 8):
            for c in range(chunk // LANES):
                rows = pl.ds(8 * r, 8)
                cols = pl.ds(at + c * LANES, LANES)
                index = bins_of(cells[pl.ds(8 + 8 * r, 8), pl.ds(at + PAD + c * LANES, LANES)]).astype(jnp.int32)
                group, lane = index >> 7, index & 127
                stretch = jnp.take_along_axis(tables[0], lane, axis=1)
                for b in range(1, 8):
                    stretch = jnp.where(group == b, jnp.take_along_axis(tables[b], lane, axis=1), stretch)
                gx = slope_x[rows, cols] * scale
                gy = slope_y[rows, cols] * scale
                light = (cos_zenith - sin_zenith * (light_x * gx + light_y * gy)) * lax.rsqrt(
                    1.0 + gx * gx + gy * gy)
                result[rows, cols] = stretch * (0.5 + jnp.maximum(light, 0.0))
        out_copy(i).start()
        return carry

    lax.fori_loop(0, chunks, finish, 0)

    @pl.when(me < n - 1)
    def _():
        down.wait_send()

    @pl.when(me > 0)
    def _():
        up.wait_send()

    def drain(k, carry):
        copy_to(k).wait_send()
        return carry

    lax.fori_loop(1, n, drain, 0)

    def flush(i, carry):
        out_copy(i).wait()
        return carry

    lax.fori_loop(0, chunks, flush, 0)


def chunk_of(width):
    chunk = 1024
    while width % chunk:
        chunk //= 2
    return chunk


def solution(mesh):
    n = mesh.shape["row"]

    def body(elevation, bin_index, ranks):
        height, width = elevation.shape
        chunk = chunk_of(width)
        grid = (height, width)
        return pl.pallas_call(
            functools.partial(kernel, n, chunk),
            out_shape=jax.ShapeDtypeStruct(grid, jnp.float32),
            in_specs=[pl.BlockSpec(memory_space=pltpu.SMEM), pl.BlockSpec(memory_space=pl.ANY)],
            out_specs=pl.BlockSpec(memory_space=pl.ANY),
            scratch_shapes=[
                pltpu.VMEM((height + 8, width + 2 * PAD), jnp.float32),
                pltpu.VMEM(grid, jnp.float32),
                pltpu.VMEM(grid, jnp.float32),
                pltpu.VMEM((10, LANES), jnp.float32),
                pltpu.VMEM((n, 10, LANES), jnp.float32),
                pltpu.VMEM(grid, jnp.float32),
                pltpu.VMEM(grid, jnp.float32),
                pltpu.VMEM(grid, jnp.float32),
                pltpu.SemaphoreType.DMA,
                pltpu.SemaphoreType.DMA((2,)),
                pltpu.SemaphoreType.DMA((2,)),
                pltpu.SemaphoreType.DMA((n,)),
                pltpu.SemaphoreType.DMA((n,)),
                pltpu.SemaphoreType.DMA((width // chunk,)),
            ],
            compiler_params=pltpu.CompilerParams(collective_id=0, has_side_effects=True),
        )(ranks, elevation)

    in_specs = (P(("groups", "row"), None), P(("groups", "row"), None), P("groups"))
    return jax.shard_map(body, mesh=mesh, in_specs=in_specs, out_specs=P(("groups", "row"), None), check_vma=False)
```

time: 618 us -> 24.4 us (0.04)
  local copies, waits for them, and re-layouts: 525 us -> 1.87 us
  blocking collectives: 65.8 us -> 0 us
  Pallas kernels: 0 us -> 22.3 us
  other arithmetic: 13.4 us -> 0 us
    gather x2 -> x0, local copies, waits for them, and re-layouts: 521 us -> none  [body(): stretch = jnp.take(table.astype(jnp.float32), bin_index, axis=0)]
    pmax x1 -> x0, blocking collectives: 36.3 us -> none  [body(): highest, neg_lowest = lax.pmax((local_max, -local_min), 'row')]
    psum x1 -> x0, blocking collectives: 29.5 us -> none  [body(): counts = lax.psum(local_counts, 'row')]
    pallas_call x0 -> x1, Pallas kernels: none -> 22.3 us  [body(): pl.pallas_call(functools.partial(kernel, n, chunk), out_shape=jax.ShapeDt...]
  transfers between devices with their start and end apart: 2 -> 0, of which waited for: 0 -> 0; matrix products, arithmetic and copies ran while one was open for 87% -> 0% of each run, Pallas kernels for 0% -> 0%
where the time goes in v1:
time: 24.4 us; the launch traced here: 24.2 us
  Pallas kernels  22.3 us (91%)
  local copies, waits for them, and re-layouts  1.87 us (8%)
    pallas_call x1, Pallas kernels, body(): pl.pallas_call(functools.partial(kernel, n, chunk), out_shape=jax.ShapeDt...  22.3 us
    unnamed x1, local copies, waits for them, and re-layouts  1.87 us

profile of v1, /device:TPU:0, one launch (start us, length us, event | category | flops | bytes accessed | tf_op | source)
XLA Modules:
  0.0 24.2 jit_solution(8384542699303593225)
XLA Ops:
  0.0 22.3 %shard_map.28 = f32[16,8192]{1,0:T(8,128)} custom-call(s32[2]{0:T(128)} %ranks_ref.1, f32[16,8192]{1,0:T(8,128)} %elev_ref.1), custom_call_target="tpu_custom_call" | custom-call | tf_op jit(solution)/shard_map/pallas_call | solution.py:277
  22.3 1.9 %copy.4 = f32[16,8192]{1,0:T(8,128)} copy(f32[16,8192]{1,0:T(8,128)} %shard_map.28) | data formatting | bytes 1048576

commit v2 on v1

--- a/solution.py
+++ b/solution.py
@@ -18,7 +18,7 @@
 PAD = 128
 SMOOTH = (1.0, 8.0, 28.0, 56.0, 70.0, 56.0, 28.0, 8.0, 1.0)
 SLOPE = (-1.0, -6.0, -14.0, -14.0, 0.0, 14.0, 14.0, 6.0, 1.0)
-UPPER = 16
+UPPER = 32
 LOWER = BINS // UPPER
 
 
@@ -26,37 +26,41 @@
     return jnp.floor(jnp.clip(cells * 0.5, 0.0, float(BINS - 1)))
 
 
-def row_weights(weights, height):
-    depth = 3 * (height + 8) + 8
-    row = lax.broadcasted_iota(jnp.int32, (height, depth), 0)
-    col = lax.broadcasted_iota(jnp.int32, (height, depth), 1)
-    own = lax.rem(col, height)
-    edge = lax.rem(jnp.maximum(col - 3 * height, 0), 8)
-    edge = jnp.where(edge < HALO, height + edge, edge - 8)
-    source = jnp.where(col < 3 * height, own, edge)
-    source = jnp.where(col < 3 * (height + 8), source, 4 * height)
+def row_weights(weights, height, halo):
+    rows = 8 if halo else height
+    row = lax.broadcasted_iota(jnp.int32, (height, 4 * rows if halo else 3 * rows), 0)
+    col = lax.broadcasted_iota(jnp.int32, row.shape, 1)
+    source = lax.rem(col, rows)
+    if halo:
+        source = jnp.where(source < HALO, height + source, source - 8)
+        source = jnp.where(col < 3 * rows, source, 4 * height)
     delta = source - row
-    out = jnp.zeros((height, depth), jnp.float32)
+    out = jnp.zeros(row.shape, jnp.float32)
     for k, weight in enumerate(weights):
         out = jnp.where(delta == k - HALO, weight, out)
     return out.astype(jnp.bfloat16)
 
 
-def split3(cells):
+def stacked(cells):
     first = cells.astype(jnp.bfloat16).astype(jnp.float32)
     rest = cells - first
     second = rest.astype(jnp.bfloat16).astype(jnp.float32)
-    return first, second, rest - second
-
-
-def stacked(cells):
-    halo = split3(cells[0:8])
-    own = split3(cells[8:])
-    return jnp.concatenate([*own, *halo, jnp.zeros_like(halo[0])], axis=0).astype(jnp.bfloat16)
-
-
-def kernel(n, chunk, ranks_ref, elev_ref, out_ref, cells, upper, lower, send, recv, slope_x, slope_y,
-           result, in_sem, halo_send, halo_recv, send_sem, recv_sem, out_sem):
+    parts = [first, second, rest - second]
+    if cells.shape[0] == 8:
+        parts.append(jnp.zeros_like(first))
+    return jnp.concatenate(parts, axis=0).astype(jnp.bfloat16)
+
+
+def columns(x):
+    wide = x.shape[1]
+    for k in range(7):
+        x = x + pltpu.roll(x, 1 if k % 2 else wide - 1, 1)
+    moved = pltpu.roll(x, 1, 1)
+    inside = slice(PAD, wide - PAD)
+    return (x - moved)[:, inside], (x + moved)[:, inside]
+
+
+def kernel(n, chunk, elev_ref, out_ref, slope_x, slope_y, cells, upper, lower, send, recv, in_sem, halo_send, halo_recv, send_sem, recv_sem):
     me = lax.axis_index("row")
     height, width = elev_ref.shape
     chunks = width // chunk
@@ -87,7 +91,6 @@
         cells[0:4, inner] = jnp.zeros((4, width), jnp.float32)
 
     load.wait()
-    pl.semaphore_wait(barrier, n - 1)
 
     down = pltpu.make_async_remote_copy(
         src_ref=cells.at[pl.ds(8 + height - HALO, HALO), inner], dst_ref=cells.at[pl.ds(4, HALO), inner],
@@ -97,14 +100,6 @@
         src_ref=cells.at[pl.ds(8, HALO), inner], dst_ref=cells.at[pl.ds(0, HALO), inner],
         send_sem=halo_send.at[1], recv_sem=halo_recv.at[1],
         device_id={"row": lax.rem(me + n - 1, n)}, device_id_type=pl.DeviceIdType.MESH)
-
-    @pl.when(me < n - 1)
-    def _():
-        down.start()
-
-    @pl.when(me > 0)
-    def _():
-        up.start()
 
     def prepare(i, carry):
         top, bottom = carry
@@ -124,7 +119,7 @@
     top, bottom = lax.fori_loop(0, chunks, prepare, (start, start))
 
     urow = lax.broadcasted_iota(jnp.int32, (UPPER, chunk), 0)
-    upper_iota = (2 * lax.rem(urow, 8) + urow // 8).astype(jnp.float32).astype(jnp.bfloat16)
+    upper_iota = (4 * lax.rem(urow, 8) + urow // 8).astype(jnp.float32).astype(jnp.bfloat16)
     lower_iota = lax.broadcasted_iota(jnp.int32, (LOWER, chunk), 0).astype(jnp.float32).astype(jnp.bfloat16)
 
     def count(i, total):
@@ -140,7 +135,7 @@
         return total
 
     total = lax.fori_loop(0, chunks, count, jnp.zeros((UPPER, LOWER), jnp.float32))
-    counts = jnp.concatenate([total[0:8], total[8:16]], axis=1)
+    counts = jnp.concatenate([total[8 * q : 8 * q + 8] for q in range(UPPER // 8)], axis=1)
     send[0:8, :] = counts
     send[8:9, :] = jnp.max(top, axis=0, keepdims=True)
     send[9:10, :] = jnp.max(-bottom, axis=0, keepdims=True)
@@ -154,33 +149,47 @@
         copy_to(k).start()
         return carry
 
+    pl.semaphore_wait(barrier, n - 1)
     lax.fori_loop(1, n, post, 0)
 
+    @pl.when(me < n - 1)
+    def _():
+        down.start()
+
     @pl.when(me > 0)
     def _():
+        up.start()
+
+
+    own_smooth, own_slope = row_weights(SMOOTH, height, False), row_weights(SLOPE, height, False)
+
+    def own_rows(i, carry):
+        at = pl.multiple_of(i * chunk, chunk)
+        rise, level = columns(cells[pl.ds(8, height), pl.ds(at, chunk + 2 * PAD)])
+        slope_x[:, pl.ds(at, chunk)] = jnp.dot(own_smooth, stacked(rise), preferred_element_type=jnp.float32)
+        slope_y[:, pl.ds(at, chunk)] = jnp.dot(own_slope, stacked(level), preferred_element_type=jnp.float32)
+        return carry
+
+    lax.fori_loop(0, chunks, own_rows, 0, unroll=2)
+
+    @pl.when(me > 0)
+    def _():
         down.wait_recv()
 
     @pl.when(me < n - 1)
     def _():
         up.wait_recv()
 
-    smooth_w = row_weights(SMOOTH, height)
-    slope_w = row_weights(SLOPE, height)
-    span_w = chunk + 2 * PAD
-
-    def stencil(i, carry):
-        at = pl.multiple_of(i * chunk, chunk)
-        x = cells[:, pl.ds(at, span_w)]
-        for k in range(7):
-            x = x + pltpu.roll(x, 1 if k % 2 else span_w - 1, 1)
-        moved = pltpu.roll(x, 1, 1)
-        rise = (x - moved)[:, PAD : PAD + chunk]
-        level = (x + moved)[:, PAD : PAD + chunk]
-        slope_x[:, pl.ds(at, chunk)] = jnp.dot(smooth_w, stacked(rise), preferred_element_type=jnp.float32)
-        slope_y[:, pl.ds(at, chunk)] = jnp.dot(slope_w, stacked(level), preferred_element_type=jnp.float32)
-        return carry
-
-    lax.fori_loop(0, chunks, stencil, 0)
+    halo_smooth, halo_slope = row_weights(SMOOTH, height, True), row_weights(SLOPE, height, True)
+
+    def halo_rows(i, carry):
+        at = pl.multiple_of(i * chunk, chunk)
+        rise, level = columns(cells[pl.ds(0, 8), pl.ds(at, chunk + 2 * PAD)])
+        slope_x[:, pl.ds(at, chunk)] += jnp.dot(halo_smooth, stacked(rise), preferred_element_type=jnp.float32)
+        slope_y[:, pl.ds(at, chunk)] += jnp.dot(halo_slope, stacked(level), preferred_element_type=jnp.float32)
+        return carry
+
+    lax.fori_loop(0, chunks, halo_rows, 0, unroll=True)
 
     def take(k, carry):
         copy_to(k).wait_recv()
@@ -188,7 +197,29 @@
         return carry[0] + got[0:8], jnp.maximum(carry[1], got[8:10])
 
     counts, ends = lax.fori_loop(1, n, take, (send[0:8, :], send[8:10, :]))
-    ends = jnp.max(ends, axis=1, keepdims=True)
+    out_ref[0:8, :] = counts
+    out_ref[8:10, :] = ends
+
+    @pl.when(me < n - 1)
+    def _():
+        down.wait_send()
+
+    @pl.when(me > 0)
+    def _():
+        up.wait_send()
+
+    def drain(k, carry):
+        copy_to(k).wait_send()
+        return carry
+
+    lax.fori_loop(1, n, drain, 0)
+
+
+def shade_kernel(chunk, ranks_ref, sums_ref, cells, slope_x, slope_y, out_ref, result, out_sem):
+    height, width = cells.shape
+    chunks = width // chunk
+    counts = sums_ref[0:8, :]
+    ends = jnp.max(sums_ref[8:10, :], axis=1, keepdims=True)
     span = ends[0:1] + ends[1:2]
     scale = jnp.broadcast_to(zfactor / (8.0 * span) * (1.0 / 4096.0), (8, LANES))
 
@@ -224,7 +255,7 @@
             for c in range(chunk // LANES):
                 rows = pl.ds(8 * r, 8)
                 cols = pl.ds(at + c * LANES, LANES)
-                index = bins_of(cells[pl.ds(8 + 8 * r, 8), pl.ds(at + PAD + c * LANES, LANES)]).astype(jnp.int32)
+                index = bins_of(cells[rows, cols]).astype(jnp.int32)
                 group, lane = index >> 7, index & 127
                 stretch = jnp.take_along_axis(tables[0], lane, axis=1)
                 for b in range(1, 8):
@@ -239,20 +270,6 @@
 
     lax.fori_loop(0, chunks, finish, 0)
 
-    @pl.when(me < n - 1)
-    def _():
-        down.wait_send()
-
-    @pl.when(me > 0)
-    def _():
-        up.wait_send()
-
-    def drain(k, carry):
-        copy_to(k).wait_send()
-        return carry
-
-    lax.fori_loop(1, n, drain, 0)
-
     def flush(i, carry):
         out_copy(i).wait()
         return carry
@@ -273,30 +290,40 @@
     def body(elevation, bin_index, ranks):
         height, width = elevation.shape
         chunk = chunk_of(width)
+        chunks = width // chunk
         grid = (height, width)
-        return pl.pallas_call(
+        room = 32 * height * width * 4
+        block = pltpu.VMEM(grid, jnp.float32)
+        whole = jax.ShapeDtypeStruct(grid, jnp.float32)
+        anywhere = pl.BlockSpec(memory_space=pl.ANY)
+        inside = pl.BlockSpec(memory_space=pltpu.VMEM)
+        sums, slope_x, slope_y = pl.pallas_call(
             functools.partial(kernel, n, chunk),
-            out_shape=jax.ShapeDtypeStruct(grid, jnp.float32),
-            in_specs=[pl.BlockSpec(memory_space=pltpu.SMEM), pl.BlockSpec(memory_space=pl.ANY)],
-            out_specs=pl.BlockSpec(memory_space=pl.ANY),
+            out_shape=[jax.ShapeDtypeStruct((10, LANES), jnp.float32), whole, whole],
+            in_specs=[anywhere],
+            out_specs=[inside, inside, inside],
             scratch_shapes=[
                 pltpu.VMEM((height + 8, width + 2 * PAD), jnp.float32),
-                pltpu.VMEM(grid, jnp.float32),
-                pltpu.VMEM(grid, jnp.float32),
+                block,
+                block,
                 pltpu.VMEM((10, LANES), jnp.float32),
                 pltpu.VMEM((n, 10, LANES), jnp.float32),
-                pltpu.VMEM(grid, jnp.float32),
-                pltpu.VMEM(grid, jnp.float32),
-                pltpu.VMEM(grid, jnp.float32),
                 pltpu.SemaphoreType.DMA,
                 pltpu.SemaphoreType.DMA((2,)),
                 pltpu.SemaphoreType.DMA((2,)),
                 pltpu.SemaphoreType.DMA((n,)),
                 pltpu.SemaphoreType.DMA((n,)),
-                pltpu.SemaphoreType.DMA((width // chunk,)),
             ],
-            compiler_params=pltpu.CompilerParams(collective_id=0, has_side_effects=True),
-        )(ranks, elevation)
+            compiler_params=pltpu.CompilerParams(collective_id=0, has_side_effects=True, vmem_limit_bytes=room),
+        )(elevation)
+        return pl.pallas_call(
+            functools.partial(shade_kernel, chunk),
+            out_shape=whole,
+            in_specs=[pl.BlockSpec(memory_space=pltpu.SMEM), inside, inside, inside, inside],
+            out_specs=anywhere,
+            scratch_shapes=[block, pltpu.SemaphoreType.DMA((chunks,))],
+            compiler_params=pltpu.CompilerParams(vmem_limit_bytes=room),
+        )(ranks, sums, elevation, slope_x, slope_y)
 
     in_specs = (P(("groups", "row"), None), P(("groups", "row"), None), P("groups"))
     return jax.shard_map(body, mesh=mesh, in_specs=in_specs, out_specs=P(("groups", "row"), None), check_vma=False)

time: 24.4 us -> 17.8 us (0.73)
  Pallas kernels: 22.3 us -> 15.9 us
    pallas_call x1 -> x2, Pallas kernels: 22.3 us -> 15.9 us  [the longest x1 12.2 us: body(): pl.pallas_call(functools.partial(kernel, n, chunk), out_shape=[jax.ShapeD...]
    unnamed x1 -> x4, local copies, waits for them, and re-layouts: 1.87 us -> 1.69 us
where the time goes in v2:
time: 17.8 us; the launch traced here: 17.6 us
  Pallas kernels  15.9 us (89%)
  local copies, waits for them, and re-layouts  1.69 us (9%)
    pallas_call x1, Pallas kernels, body(): pl.pallas_call(functools.partial(kernel, n, chunk), out_shape=[jax.ShapeD...  12.2 us
    pallas_call x1, Pallas kernels, body(): pl.pallas_call(functools.partial(shade_kernel, chunk), out_shape=whole, i...  3.77 us
    unnamed x4, local copies, waits for them, and re-layouts  1.69 us

profile of v2, /device:TPU:0, one launch (start us, length us, event | category | flops | bytes accessed | tf_op | source)
XLA Modules:
  0.0 17.6 jit_solution(3057669446018351849)
XLA Ops:
  0.0 0.0 copy-start
  0.0 1.0 %copy-done = f32[16,8192]{1,0:T(8,128)S(1)} copy-done((f32[16,8192]{1,0:T(8,128)S(1)}, f32[16,8192]{1,0:T(8,128)}, u32[]{:S(2)}) %copy-start) | copy-done | bytes 524312
  1.0 12.2 %shard_map.28 = (f32[10,128]{1,0:T(8,128)S(1)}, f32[16,8192]{1,0:T(8,128)S(1)}, f32[16,8192]{1,0:T(8,128)S(1)}) custom-call(f32[16,8192]{1,0:T(8,128)S(1)} %copy-done), custom_call_target="tpu_custom_call" | custom-call | tf_op jit(solution)/shard_map/pallas_call | solution.py:300
  13.2 0.0 copy-start.1
  13.2 0.6 %copy-done.1 = s32[2]{0:T(128)S(1)} copy-done((s32[2]{0:T(128)S(1)}, s32[2]{0:T(128)}, u32[]{:S(2)}) %copy-start.1) | copy-done | bytes 32
  13.9 3.8 %shard_map.29 = f32[16,8192]{1,0:T(8,128)} custom-call(s32[2]{0:T(128)S(1)} %copy-done.1, f32[10,128]{1,0:T(8,128)S(1)} %get-tuple-element.8.sums_ref, f32[16,8192]{1,0:T(8,128)S(1)} %copy-done, f32[16,8192]{1,0:T(8,128)S(1)} %get-tuple-element.9.slope_x, f32[16,8192]{1,0:T(8,128)S(1)} %get-tuple-element.10.slope_y), custom_call_target="tpu_custom_call" | custom-call | tf_op jit(solution)/shard_map/pallas_call | solution.py:319
Async XLA Ops:
  0.0 1.0 %copy-start = (f32[16,8192]{1,0:T(8,128)S(1)}, f32[16,8192]{1,0:T(8,128)}, u32[]{:S(2)}) copy-start(f32[16,8192]{1,0:T(8,128)} %cells.1) | copy-start | bytes 1572868
  13.2 0.7 %copy-start.1 = (s32[2]{0:T(128)S(1)}, s32[2]{0:T(128)}, u32[]{:S(2)}) copy-start(s32[2]{0:T(128)} %ranks_ref.1) | copy-start | bytes 28

commit v3 on v2

--- a/solution.py
+++ b/solution.py
@@ -60,7 +60,7 @@
     return (x - moved)[:, inside], (x + moved)[:, inside]
 
 
-def kernel(n, chunk, elev_ref, out_ref, slope_x, slope_y, cells, upper, lower, send, recv, in_sem, halo_send, halo_recv, send_sem, recv_sem):
+def kernel(n, chunk, ranks_ref, elev_ref, out_ref, index, slope_x, slope_y, cells, upper, lower, send, recv, ranks, in_sem, rank_sem, halo_send, halo_recv, send_sem, recv_sem):
     me = lax.axis_index("row")
     height, width = elev_ref.shape
     chunks = width // chunk
@@ -68,6 +68,8 @@
 
     load = pltpu.make_async_copy(elev_ref, cells.at[pl.ds(8, height), inner], in_sem)
     load.start()
+    rank_load = pltpu.make_async_copy(ranks_ref, ranks, rank_sem)
+    rank_load.start()
 
     barrier = pltpu.get_barrier_semaphore()
 
@@ -106,6 +108,7 @@
         at = pl.multiple_of(i * chunk, chunk)
         block = cells[pl.ds(8, height), pl.ds(at + PAD, chunk)]
         bins = bins_of(block)
+        index[:, pl.ds(at, chunk)] = bins.astype(jnp.int32)
         high = jnp.floor(bins * (1.0 / LOWER))
         upper[:, pl.ds(at, chunk)] = high
         lower[:, pl.ds(at, chunk)] = bins - high * LOWER
@@ -197,29 +200,7 @@
         return carry[0] + got[0:8], jnp.maximum(carry[1], got[8:10])
 
     counts, ends = lax.fori_loop(1, n, take, (send[0:8, :], send[8:10, :]))
-    out_ref[0:8, :] = counts
-    out_ref[8:10, :] = ends
-
-    @pl.when(me < n - 1)
-    def _():
-        down.wait_send()
-
-    @pl.when(me > 0)
-    def _():
-        up.wait_send()
-
-    def drain(k, carry):
-        copy_to(k).wait_send()
-        return carry
-
-    lax.fori_loop(1, n, drain, 0)
-
-
-def shade_kernel(chunk, ranks_ref, sums_ref, cells, slope_x, slope_y, out_ref, result, out_sem):
-    height, width = cells.shape
-    chunks = width // chunk
-    counts = sums_ref[0:8, :]
-    ends = jnp.max(sums_ref[8:10, :], axis=1, keepdims=True)
+    ends = jnp.max(ends, axis=1, keepdims=True)
     span = ends[0:1] + ends[1:2]
     scale = jnp.broadcast_to(zfactor / (8.0 * span) * (1.0 / 4096.0), (8, LANES))
 
@@ -233,7 +214,8 @@
     within = sums[0:8] + 256.0 * sums[8:16] + 65536.0 * sums[16:24]
     before = jnp.zeros((1, 1), jnp.float32)
     rows = []
-    first, second = ranks_ref[0], ranks_ref[1]
+    rank_load.wait()
+    first, second = ranks[0], ranks[1]
     for b in range(8):
         rows.append(before)
         before = before + within[b : b + 1, LANES - 1 : LANES]
@@ -242,6 +224,29 @@
     divisor = jnp.full((8, LANES), second - first, jnp.int32).astype(jnp.float32)
     table = jnp.clip((cumulative - first).astype(jnp.float32) / divisor, 0.0, 1.0)
     table = table.astype(jnp.bfloat16).astype(jnp.float32)
+    out_ref[0:8, :] = table
+    out_ref[8:16, :] = scale
+
+    @pl.when(me < n - 1)
+    def _():
+        down.wait_send()
+
+    @pl.when(me > 0)
+    def _():
+        up.wait_send()
+
+    def drain(k, carry):
+        copy_to(k).wait_send()
+        return carry
+
+    lax.fori_loop(1, n, drain, 0)
+
+
+def shade_kernel(chunk, sums_ref, index_ref, slope_x, slope_y, out_ref, result, out_sem):
+    height, width = index_ref.shape
+    chunks = width // chunk
+    table = sums_ref[0:8, :]
+    scale = sums_ref[8:16, :]
     tables = [jnp.broadcast_to(table[b : b + 1], (8, LANES)) for b in range(8)]
 
     def out_copy(i):
@@ -255,8 +260,8 @@
             for c in range(chunk // LANES):
                 rows = pl.ds(8 * r, 8)
                 cols = pl.ds(at + c * LANES, LANES)
-                index = bins_of(cells[rows, cols]).astype(jnp.int32)
-                group, lane = index >> 7, index & 127
+                which = index_ref[rows, cols]
+                group, lane = which >> 7, which & 127
                 stretch = jnp.take_along_axis(tables[0], lane, axis=1)
                 for b in range(1, 8):
                     stretch = jnp.where(group == b, jnp.take_along_axis(tables[b], lane, axis=1), stretch)
@@ -297,17 +302,19 @@
         whole = jax.ShapeDtypeStruct(grid, jnp.float32)
         anywhere = pl.BlockSpec(memory_space=pl.ANY)
         inside = pl.BlockSpec(memory_space=pltpu.VMEM)
-        sums, slope_x, slope_y = pl.pallas_call(
+        sums, index, slope_x, slope_y = pl.pallas_call(
             functools.partial(kernel, n, chunk),
-            out_shape=[jax.ShapeDtypeStruct((10, LANES), jnp.float32), whole, whole],
-            in_specs=[anywhere],
-            out_specs=[inside, inside, inside],
+            out_shape=[jax.ShapeDtypeStruct((16, LANES), jnp.float32), jax.ShapeDtypeStruct(grid, jnp.int32), whole, whole],
+            in_specs=[anywhere, pl.BlockSpec(memory_space=pltpu.HBM)],
+            out_specs=[inside] * 4,
             scratch_shapes=[
                 pltpu.VMEM((height + 8, width + 2 * PAD), jnp.float32),
                 block,
                 block,
                 pltpu.VMEM((10, LANES), jnp.float32),
                 pltpu.VMEM((n, 10, LANES), jnp.float32),
+                pltpu.SMEM((2,), jnp.int32),
+                pltpu.SemaphoreType.DMA,
                 pltpu.SemaphoreType.DMA,
                 pltpu.SemaphoreType.DMA((2,)),
                 pltpu.SemaphoreType.DMA((2,)),
@@ -315,15 +322,15 @@
                 pltpu.SemaphoreType.DMA((n,)),
             ],
             compiler_params=pltpu.CompilerParams(collective_id=0, has_side_effects=True, vmem_limit_bytes=room),
-        )(elevation)
+        )(ranks, elevation)
         return pl.pallas_call(
             functools.partial(shade_kernel, chunk),
             out_shape=whole,
-            in_specs=[pl.BlockSpec(memory_space=pltpu.SMEM), inside, inside, inside, inside],
+            in_specs=[inside] * 4,
             out_specs=anywhere,
             scratch_shapes=[block, pltpu.SemaphoreType.DMA((chunks,))],
             compiler_params=pltpu.CompilerParams(vmem_limit_bytes=room),
-        )(ranks, sums, elevation, slope_x, slope_y)
+        )(sums, index, slope_x, slope_y)
 
     in_specs = (P(("groups", "row"), None), P(("groups", "row"), None), P("groups"))
     return jax.shard_map(body, mesh=mesh, in_specs=in_specs, out_specs=P(("groups", "row"), None), check_vma=False)

time: 17.8 us -> 17.2 us (0.966)
  Pallas kernels: 15.9 us -> 15.3 us
    pallas_call x1, Pallas kernels: 3.77 us -> 2.89 us  [body(): pl.pallas_call(functools.partial(shade_kernel, chunk), out_shape=whole, i...]
    pallas_call x1, Pallas kernels: 12.2 us -> 12.5 us  [body(): pl.pallas_call(functools.partial(kernel, n, chunk), out_shape=[jax.ShapeD...]
where the time goes in v3:
time: 17.2 us; the launch traced here: 17.1 us
  Pallas kernels  15.3 us (89%)
  local copies, waits for them, and re-layouts  1.7 us (10%)
    pallas_call x1, Pallas kernels, body(): pl.pallas_call(functools.partial(kernel, n, chunk), out_shape=[jax.ShapeD...  12.5 us
    pallas_call x1, Pallas kernels, body(): pl.pallas_call(functools.partial(shade_kernel, chunk), out_shape=whole, i...  2.89 us
    unnamed x4, local copies, waits for them, and re-layouts  1.7 us

profile of v3, /device:TPU:0, one launch (start us, length us, event | category | flops | bytes accessed | tf_op | source)
XLA Modules:
  0.0 17.1 jit_solution(6698733915612389399)
XLA Ops:
  0.0 0.0 copy-start
  0.0 1.0 %copy-done = f32[16,8192]{1,0:T(8,128)S(1)} copy-done((f32[16,8192]{1,0:T(8,128)S(1)}, f32[16,8192]{1,0:T(8,128)}, u32[]{:S(2)}) %copy-start) | copy-done | bytes 524312
  1.0 0.0 copy-start.1
  1.0 0.7 %copy-done.1 = s32[2]{0:T(128)S(1)} copy-done((s32[2]{0:T(128)S(1)}, s32[2]{0:T(128)}, u32[]{:S(2)}) %copy-start.1) | copy-done | bytes 32
  1.7 12.5 %shard_map.28 = (f32[16,128]{1,0:T(8,128)S(1)}, s32[16,8192]{1,0:T(8,128)S(1)}, f32[16,8192]{1,0:T(8,128)S(1)}, f32[16,8192]{1,0:T(8,128)S(1)}) custom-call(s32[2]{0:T(128)S(1)} %copy-done.1, f32[16,8192]{1,0:T(8,128)S(1)} %copy-done), custom_call_target="tpu_custom_call" | custom-call | tf_op jit(solution)/shard_map/pallas_call | solution.py:305
  14.2 2.9 %shard_map.29 = f32[16,8192]{1,0:T(8,128)} custom-call(f32[16,128]{1,0:T(8,128)S(1)} %get-tuple-element.9.sums_ref, s32[16,8192]{1,0:T(8,128)S(1)} %get-tuple-element.10.index_ref, f32[16,8192]{1,0:T(8,128)S(1)} %get-tuple-element.11.slope_x, f32[16,8192]{1,0:T(8,128)S(1)} %get-tuple-element.12.slope_y), custom_call_target="tpu_custom_call" | custom-call | tf_op jit(solution)/shard_map/pallas_call | solution.py:326
Async XLA Ops:
  0.0 1.0 %copy-start = (f32[16,8192]{1,0:T(8,128)S(1)}, f32[16,8192]{1,0:T(8,128)}, u32[]{:S(2)}) copy-start(f32[16,8192]{1,0:T(8,128)} %elev_ref.1) | copy-start | bytes 1572868
  1.0 0.7 %copy-start.1 = (s32[2]{0:T(128)S(1)}, s32[2]{0:T(128)}, u32[]{:S(2)}) copy-start(s32[2]{0:T(128)} %ranks_ref.1) | copy-start | bytes 28
